TPU v7x, 32 devices: a whole 2x2x4 slice. The times are simulated.
32 devices in a mesh: dp: 4 (over y, core), seq: 2 (over x), expert: 4 (over z).
Axes of the slice: x: 2, y: 2, z: 4, core: 2. Of those that a mesh axis runs over, the one named last changes fastest.
Arguments:
- queries: bfloat16 [512, 4096], P(('dp', 'seq'), 'expert'), parts along dimension 0, may hold values from -256 to 256, as said below
- keys: bfloat16 [2048, 1024], P(('dp', 'seq'), 'expert'), parts along dimension 0, may hold values from -6 to 6
- values: bfloat16 [2048, 1024], P(('dp', 'seq'), 'expert'), parts along dimension 0, may hold values from -6 to 6
- lengths: int32 [32], P('dp'), parts along dimension 0, may hold values from 1 to 256, 512 in all
- routes: int32 [512, 2], P(('dp', 'seq', 'expert')), parts along dimension 0, may hold values from 0 to 3, all different within a row; in each aligned block of 16 rows (0 to 15, 16 to 31, ...) at most 12 rows name the same one
- gates: float32 [512, 2], P(('dp', 'seq', 'expert')), parts along dimension 0, may hold values from 0.2 to 1
- w_up: bfloat16 [4, 4096, 7168], P('expert', None, 'seq'), may hold values from -0.09375 to 0.09375
Outputs:
- expert_mix: bfloat16 [512, 7168], P(('dp', 'seq', 'expert')), parts along dimension 0
There are 4 independent parts, one for each index of `dp`. A program takes and returns all parts, laid end to end along the dimension named above; an argument that names none is the same for every part. Nothing has to cross between parts.
Inputs may be any that keep to these rules, and one draw needn't show every extreme that they name: `queries`: A query row's values are those of a normal draw or, in some rows, a multiple of a sum of key rows. The 8 lengths sum to 512. `routes`: A row's two experts differ; among the 16 rows of one device no expert is named more than 12 times.
All inputs are finite; a program needn't handle non-finite values.
Results may differ from a plain program's by a relative error of at most 0.012.
Values may be sent and summed in bfloat16 or wider, within the bound.
A program may use at most 64 MiB of HBM per device.

v0:
```python
import jax
import jax.numpy as jnp
from jax import lax
from jax.sharding import PartitionSpec as P

HD = 128


def doc_index(positions, starts):
    return jnp.sum((positions[:, None] >= starts[None, :]).astype(jnp.int32), axis=1) - 1


def shards(queries, keys, values, lengths, routes, gates, w_up):
    q_rows, width = queries.shape
    shard_len = keys.shape[0]
    kv_local = keys.shape[1] // HD
    group = width // HD // kv_local
    scale = 1.0 / HD**0.5
    seq_count = lax.axis_size("seq")
    expert_count = lax.axis_size("expert")
    experts_all = expert_count * w_up.shape[0]
    capacity = max(2, 3 * q_rows // (expert_count * expert_count))
    starts = jnp.cumsum(lengths) - lengths
    qpos = (
        lax.axis_index("seq") * shard_len + shard_len - q_rows + jnp.arange(q_rows, dtype=jnp.int32)
    )
    qdoc = doc_index(qpos, starts)
    q_split = queries.reshape(q_rows, kv_local, group, HD)
    start_peak = jnp.full((kv_local, group, q_rows), -1e30, jnp.float32)
    peak = start_peak
    k_piece = lax.all_gather(keys, "seq", axis=0, tiled=True)
    v_piece = lax.all_gather(values, "seq", axis=0, tiled=True)
    count = k_piece.shape[0]
    kpos = jnp.arange(count, dtype=jnp.int32)
    allowed = (kpos[None, :] <= qpos[:, None]) & (doc_index(kpos, starts)[None, :] == qdoc[:, None])
    score = (
        jnp.einsum(
            "qkgd,pkd->kgqp",
            q_split,
            k_piece.reshape(count, kv_local, HD),
            preferred_element_type=jnp.float32,
        )
        * scale
    )
    masked = jnp.where(allowed, score, jnp.float32(-1e30))
    new_peak = jnp.maximum(peak, jnp.max(masked, axis=-1))
    weight = jnp.where(allowed, jnp.exp(score - new_peak[..., None]), jnp.float32(0.0))
    total = jnp.sum(weight, axis=-1)
    update = jnp.einsum(
        "kgqp,pkd->kgqd",
        weight.astype(jnp.bfloat16),
        v_piece.reshape(count, kv_local, HD),
        preferred_element_type=jnp.float32,
    )
    peak, total, acc = (new_peak, total, update)
    attended = (
        (acc / total[..., None]).astype(jnp.bfloat16).transpose(2, 0, 1, 3).reshape(q_rows, width)
    )
    tok_feats = lax.all_to_all(attended, "expert", split_axis=0, concat_axis=1, tiled=True)
    feats = tok_feats.astype(jnp.float32)
    normed = (feats * lax.rsqrt(jnp.mean(feats * feats, axis=-1, keepdims=True) + 1e-05)).astype(
        jnp.bfloat16
    )
    flat = routes.reshape(-1)
    onehot = (flat[:, None] == jnp.arange(experts_all, dtype=jnp.int32)[None, :]).astype(jnp.int32)
    before = jnp.cumsum(onehot, axis=0) - onehot
    slot = jnp.sum(before * onehot, axis=1)
    target = flat * capacity + slot
    selector = (
        jnp.arange(experts_all * capacity, dtype=jnp.int32)[:, None] == target[None, :]
    ).astype(jnp.bfloat16)
    repeated = jnp.repeat(normed, 2, axis=0)
    outgoing = jnp.dot(selector, repeated, preferred_element_type=jnp.float32).astype(jnp.bfloat16)
    copies = jnp.broadcast_to(outgoing[None], (seq_count,) + outgoing.shape).reshape(
        seq_count * outgoing.shape[0], outgoing.shape[1]
    )
    incoming = lax.all_to_all(copies, ("seq", "expert"), split_axis=0, concat_axis=0, tiled=True)
    upper = jnp.dot(incoming, w_up[0], preferred_element_type=jnp.float32)
    act = jax.nn.silu(upper).astype(jnp.bfloat16)
    ff_local = act.shape[1]
    back = lax.all_to_all(act, ("seq", "expert"), split_axis=0, concat_axis=0, tiled=True)
    back = back.reshape(seq_count, experts_all, capacity, ff_local).transpose(1, 2, 0, 3)
    returned = back.reshape(experts_all * capacity, seq_count * ff_local)
    picked = jnp.dot(selector.T, returned, preferred_element_type=jnp.float32)
    tok_count = routes.shape[0]
    mixed = jnp.sum(picked.reshape(tok_count, 2, -1) * gates[:, :, None], axis=1)
    return mixed.astype(jnp.bfloat16)


def solution(mesh):
    placed = (
        P(("dp", "seq"), "expert"),
        P(("dp", "seq"), "expert"),
        P(("dp", "seq"), "expert"),
        P("dp"),
        P(("dp", "seq", "expert"), None),
        P(("dp", "seq", "expert"), None),
        P("expert", None, "seq"),
    )
    return jax.shard_map(
        shards,
        mesh=mesh,
        in_specs=placed,
        out_specs=P(("dp", "seq", "expert"), None),
        check_vma=False,
    )
```

profile of v0, /device:TPU:0, one launch (start us, length us, event | category | flops | bytes accessed | tf_op | source)
XLA Modules:
  0.0 98.6 jit_solution(351214801436123509)
XLA Ops:
  0.0 0.9 reduce-window.9
  0.9 0.7 bitcast_subtract_fusion
  1.7 1.0 %copy.22 = bf16[256,256]{0,1:T(8,128)(2,1)S(1)} copy(bf16[256,256]{1,0:T(8,128)(2,1)} %param.8) | data formatting | bytes 262144 | tf_op args[1]
  2.7 7.1 %all_gather.6 = bf16[512,256]{0,1:T(8,128)(2,1)S(1)} all-gather(bf16[256,256]{0,1:T(8,128)(2,1)S(1)} %copy.22), channel_id=1, replica_groups=mesh['dp'=4,'seq'=2,'expert'=4] {'seq'}, dimensions={0}, use_global_device_ids=true | all-gather | bytes 393216 | tf_op jit(solution)/shard_map/all_gather | solution.py:31
  9.8 1.0 reshape.125
  10.9 0.4 select_reduce_fusion
  11.4 5.6 %all_gather.7 = bf16[512,256]{0,1:T(8,128)(2,1)S(1)} all-gather(bf16[256,256]{0,1:T(8,128)(2,1)S(1)} %copy.25), channel_id=1, replica_groups=mesh['dp'=4,'seq'=2,'expert'=4] {'seq'}, dimensions={0}, use_global_device_ids=true | all-gather | bytes 393216 | tf_op jit(solution)/shard_map/all_gather | solution.py:32
  17.1 0.3 fusion.8
  17.4 0.4 fusion.7
  17.9 0.7 all_to_all.24
  18.7 5.1 %all-to-all-start = ((bf16[4,16,1024]{2,1,0:T(8,128)(2,1)}), bf16[4,16,1024]{2,1,0:T(8,128)(2,1)S(1)}, u32[]{:S(2)}, u32[]{:S(2)}) async-start(bf16[4,16,1024]{2,1,0:T(8,128)(2,1)} %all_to_all.24), calls=%async_computation | async-start | bytes 262144 | tf_op jit(solution)/shard_map/all_to_all | solution.py:59
  24.1 0.2 select_reduce_fusion.1
  24.3 5.4 %all-to-all-done = bf16[4,16,1024]{2,1,0:T(8,128)(2,1)S(1)} async-done(((bf16[4,16,1024]{2,1,0:T(8,128)(2,1)}), bf16[4,16,1024]{2,1,0:T(8,128)(2,1)S(1)}, u32[]{:S(2)}, u32[]{:S(2)}) %all-to-all-start) | async-done | bytes 131104 | tf_op jit(solution)/shard_map/all_to_all | solution.py:59
  30.0 0.2 broadcast_in_dim.22
  30.3 0.2 convolution_convert_fusion
  30.6 0.2 all_to_all.26
  30.8 26.8 %all_to_all.34 = bf16[8,12,4096]{2,1,0:T(8,128)(2,1)S(1)} all-to-all(bf16[8,12,4096]{2,1,0:T(8,128)(2,1)S(1)} %all_to_all.26), channel_id=1, replica_groups=mesh['dp'=4,'seq'=2,'expert'=4] {'seq','expert'}, dimensions={0} | all-to-all | bytes 1572864 | tf_op jit(solution)/shard_map/all_to_all | solution.py:77
  57.8 12.2 %multiply_convert_fusion = bf16[96,3584]{1,0:T(8,128)(2,1)S(1)} fusion(bf16[96,4096]{1,0:T(8,128)(2,1)S(1)} %all_to_all.28, bf16[1,4096,3584]{2,1,0:T(8,128)(2,1)} %param.13), kind=kOutput, calls=%fused_computation.4 | convolution fusion | flops 2820292608 | bytes 30834688 | tf_op jit(solution)/shard_map/dot_general | solution.py:78
  70.0 1.1 %all_to_all.29 = bf16[8,12,3584]{2,1,0:T(8,128)(2,1)} reshape(bf16[96,3584]{1,0:T(8,128)(2,1)S(1)} %multiply_convert_fusion) | data formatting | bytes 1376256 | tf_op jit(solution)/shard_map/all_to_all | solution.py:81
  71.1 3.6 %all-to-all-start.2 = ((bf16[8,12,3584]{2,1,0:T(8,128)(2,1)}), bf16[8,12,3584]{2,1,0:T(8,128)(2,1)S(1)}, u32[]{:S(2)}, u32[]{:S(2)}) async-start(bf16[8,12,3584]{2,1,0:T(8,128)(2,1)} %all_to_all.29), calls=%async_computation.2 | async-start | bytes 1835008 | tf_op jit(solution)/shard_map/all_to_all | solution.py:81
  74.7 21.6 %all-to-all-done.2 = bf16[8,12,3584]{2,1,0:T(8,128)(2,1)S(1)} async-done(((bf16[8,12,3584]{2,1,0:T(8,128)(2,1)}), bf16[8,12,3584]{2,1,0:T(8,128)(2,1)S(1)}, u32[]{:S(2)}, u32[]{:S(2)}) %all-to-all-start.2) | async-done | bytes 688160 | tf_op jit(solution)/shard_map/all_to_all | solution.py:81
  96.4 0.7 copy.45
  97.1 0.5 reshape.133
  97.6 1.0 fusion.5
  (30 shorter events, 1.5 us)
Async XLA Ops:
  0.0 11.3 %copy-start = (bf16[256,256]{1,0:T(8,128)(2,1)S(1)}, bf16[256,256]{1,0:T(8,128)(2,1)}, u32[]{:S(2)}) copy-start(bf16[256,256]{1,0:T(8,128)(2,1)} %param.9) | copy-start | bytes 393220
  17.4 6.4 %copy-start.1 = (s32[16,2]{0,1:T(2,128)S(1)}, s32[16,2]{0,1:T(2,128)}, u32[]{:S(2)}) copy-start(s32[16,2]{0,1:T(2,128)} %param.11) | copy-start | bytes 388
  18.7 11.0 %all-to-all-start = ((bf16[4,16,1024]{2,1,0:T(8,128)(2,1)}), bf16[4,16,1024]{2,1,0:T(8,128)(2,1)S(1)}, u32[]{:S(2)}, u32[]{:S(2)}) async-start(bf16[4,16,1024]{2,1,0:T(8,128)(2,1)} %all_to_all.24), calls=%async_computation | async-start | bytes 262144 | tf_op jit(solution)/shard_map/all_to_all | solution.py:59
  71.1 25.3 %all-to-all-start.2 = ((bf16[8,12,3584]{2,1,0:T(8,128)(2,1)}), bf16[8,12,3584]{2,1,0:T(8,128)(2,1)S(1)}, u32[]{:S(2)}, u32[]{:S(2)}) async-start(bf16[8,12,3584]{2,1,0:T(8,128)(2,1)} %all_to_all.29), calls=%async_computation.2 | async-start | bytes 1835008 | tf_op jit(solution)/shard_map/all_to_all | solution.py:81
  96.4 1.3 %copy-start.2 = (f32[16,2]{0,1:T(2,128)S(1)}, f32[16,2]{0,1:T(2,128)}, u32[]{:S(2)}) copy-start(f32[16,2]{0,1:T(2,128)} %param.12) | copy-start | bytes 388
where the time goes:
time: 99 us; the launch traced here: 98.6 us
  blocking collectives  39.5 us (40%)
  waiting for transfers between devices  27 us (27%)
  matrix products  14.2 us (14%)
  starting transfers between devices  8.68 us (9%)
  local copies, waits for them, and re-layouts  6.17 us (6%)
  other arithmetic  2.8 us (3%)
    all_to_all x1, blocking collectives, shards(): lax.all_to_all(copies, ('seq', 'expert'), split_axis=0, concat_axis=0, ti...  26.8 us
    all_to_all x1, waiting for transfers between devices, shards(): lax.all_to_all(act, ('seq', 'expert'), split_axis=0, concat_axis=0, tiled...  21.6 us
    dot_general x1, matrix products, shards(): upper = jnp.dot(incoming, w_up[0], preferred_element_type=jnp.float32)  12.2 us
    all_gather x1, blocking collectives, shards(): k_piece = lax.all_gather(keys, 'seq', axis=0, tiled=True)  7.12 us
    all_gather x1, blocking collectives, shards(): v_piece = lax.all_gather(values, 'seq', axis=0, tiled=True)  5.64 us
    all_to_all x1, waiting for transfers between devices, shards(): lax.all_to_all(attended, 'expert', split_axis=0, concat_axis=1, tiled=True)  5.42 us
    all_to_all x1, starting transfers between devices, shards(): lax.all_to_all(attended, 'expert', split_axis=0, concat_axis=1, tiled=True)  5.13 us
    all_to_all x1, starting transfers between devices, shards(): lax.all_to_all(act, ('seq', 'expert'), split_axis=0, concat_axis=0, tiled...  3.55 us
  transfers between devices with their start and end apart: 2, of which 2 were waited for; matrix products, arithmetic and copies ran while one was open for 1% of the time, Pallas kernels for 0%

commit v1 on v0

v1 whole, which is shorter than its diff:
```python
import functools

import jax
import jax.numpy as jnp
from jax import lax
from jax.experimental import pallas as pl
from jax.experimental.pallas import tpu as pltpu
from jax.sharding import PartitionSpec as P

HD = 128
MESH = pl.DeviceIdType.MESH
F32 = jnp.float32
BF16 = jnp.bfloat16
NT = (((1,), (1,)), ((), ()))


def up(n, m):
    return -(-n // m) * m


def iota(shape, dim):
    return lax.broadcasted_iota(jnp.int32, shape, dim)


def onehot(mask):
    return jnp.where(mask, F32(1.0), F32(0.0)).astype(BF16)


def dot(a, b):
    return jnp.dot(a, b, preferred_element_type=F32)


def kernel(
    cfg,
    len_ref, q_ref, k_ref, v_ref, routes_ref, gates_ref, w_hbm, out_ref,
    wbuf, kbuf, vbuf, rbuf, pack, xbuf, acc, sendbuf, recv,
    w_sem, kv_send, kv_recv, r_send, r_recv, z_send, z_recv, x_send, x_recv,
    own_sem, b_send, b_recv,
):
    S, E, ndoc, cap, RB, F, RP, nc, steps, pieces, tile = cfg
    s = lax.axis_index("seq")
    e = lax.axis_index("expert")
    q_rows, width = q_ref.shape
    shard = k_ref.shape[0]
    kvl = k_ref.shape[1] // HD
    group = width // HD // kvl
    T = routes_ref.shape[0]
    ff = w_hbm.shape[1]
    depth = w_hbm.shape[0]
    scale = 1.0 / HD**0.5
    rows = S * RB

    def at_s(d):
        return lax.rem(s + S - d, S)

    def at_e(d):
        return lax.rem(e + E - d, E)

    barrier = pltpu.get_barrier_semaphore()
    for ds in range(S):
        for de in range(E):
            if ds or de:
                pl.semaphore_signal(
                    barrier, inc=1, device_id={"seq": at_s(ds), "expert": at_e(de)},
                    device_id_type=MESH,
                )

    def w_copy(r):
        src = lax.rem(e + r, E)
        return pltpu.make_async_copy(
            w_hbm.at[pl.ds(pl.multiple_of(src * width, width), width)], wbuf.at[r], w_sem.at[r]
        )

    for r in range(E):
        w_copy(r).start()
    pl.semaphore_wait(barrier, S * E - 1)

    def remote(src, dst, ssem, rsem, ds, de):
        return pltpu.make_async_remote_copy(
            src_ref=src, dst_ref=dst, send_sem=ssem, recv_sem=rsem,
            device_id={"seq": at_s(ds), "expert": at_e(de)}, device_id_type=MESH,
        )

    kv_copies = []
    offset = 0
    for i, (d, first) in enumerate(pieces):
        n = shard - first
        kc = remote(k_ref.at[pl.ds(first, n)], kbuf.at[pl.ds(offset, n)],
                    kv_send.at[2 * i], kv_recv.at[2 * i], S - d, 0)
        vc = remote(v_ref.at[pl.ds(first, n)], vbuf.at[pl.ds(offset, n)],
                    kv_send.at[2 * i + 1], kv_recv.at[2 * i + 1], S - d, 0)
        kc.start()
        vc.start()
        kv_copies += [kc, vc]
        offset += n
    r_copies = []
    for de in range(1, E):
        c = remote(routes_ref, rbuf.at[de], r_send.at[de], r_recv.at[de], 0, de)
        c.start()
        r_copies.append(c)

    qn = group * q_rows
    qpos = s * shard + shard - q_rows + lax.rem(iota((qn, 1), 0), q_rows)
    docstart = jnp.zeros((qn, 1), jnp.int32)
    begin = jnp.int32(0)
    for j in range(ndoc):
        docstart = jnp.where(qpos >= begin, begin, docstart)
        begin = begin + len_ref[j]

    def masked(q, k, first):
        sc = lax.dot_general(q, k, NT, preferred_element_type=F32) * scale
        kpos = first + iota((1, k.shape[0]), 1)
        return jnp.where((kpos <= qpos) & (kpos >= docstart), sc, F32(-1e30))

    queries = []
    local = []
    for h in range(kvl):
        q = jnp.concatenate(
            [q_ref[:, (h * group + g) * HD:(h * group + g + 1) * HD] for g in range(group)], axis=0
        )
        queries.append(q)
        local.append(masked(q, k_ref[:, h * HD:(h + 1) * HD], s * shard))

    for c in r_copies:
        c.wait()
    lanes = iota((1, 128), 1)
    mine = routes_ref[...]

    def members(rt):
        return onehot((rt[:, 0:1] == lanes) | (rt[:, 1:2] == lanes))

    eye = onehot(iota((up(E, 8), 128), 0) == iota((up(E, 8), 128), 1))
    upper = onehot(iota((T, T), 0) < iota((T, T), 1))
    blocks = []
    for de in range(E):
        m = members(mine if de == 0 else rbuf[de])
        mt = lax.dot_general(eye, m, NT, preferred_element_type=F32)
        cnt = dot(mt.astype(BF16), upper)
        blk = lax.rem(e + de, E)
        place = jnp.where(mt > 0.5, cnt + (blk * cap).astype(F32), F32(-1.0))
        blocks.append((place, blk))
    Q = q_rows
    total_place = jnp.zeros((up(E, 8), Q), F32)
    for place, blk in blocks:
        shift = onehot(iota((T, Q), 0) + blk * T == iota((T, Q), 1))
        total_place = total_place + dot((place + 1.0).astype(BF16), shift)
    row_of = iota((RB, Q), 0).astype(F32) + 1.0
    sel = []
    for x in range(E):
        sel.append(onehot(total_place[x:x + 1, :] == row_of))
    selector = jnp.concatenate(sel, axis=0)

    for c in kv_copies:
        c.wait()
    for h in range(kvl):
        q = queries[h]
        hs = slice(h * HD, (h + 1) * HD)
        parts = [(local[h], v_ref[:, hs])]
        offset = 0
        for d, first in pieces:
            n = shard - first
            parts.append((masked(q, kbuf[offset:offset + n, hs], (s - d) * shard + first),
                          vbuf[offset:offset + n, hs]))
            offset += n
        peak = jnp.max(parts[0][0], axis=-1, keepdims=True)
        for sc, _ in parts[1:]:
            peak = jnp.maximum(peak, jnp.max(sc, axis=-1, keepdims=True))
        total, got = None, None
        for sc, v in parts:
            wt = jnp.exp(sc - peak)
            t = jnp.sum(wt, axis=-1, keepdims=True)
            o = dot(wt.astype(BF16), v)
            total = t if total is None else total + t
            got = o if got is None else got + o
        att = (got / total).astype(BF16)
        for g in range(group):
            cols = slice((h * group + g) * HD, (h * group + g + 1) * HD)
            packed = dot(selector, att[g * q_rows:(g + 1) * q_rows]).astype(BF16)
            for x in range(E):
                pack[x, :, cols] = packed[x * RB:(x + 1) * RB]

    mine_rows = pl.ds(pl.multiple_of(s * RB, RB), RB)

    z_copies = [None]
    for r in range(1, E):
        c = remote(pack.at[at_e(r)], xbuf.at[r, mine_rows], z_send.at[r], z_recv.at[r], 0, r)
        c.start()
        z_copies.append(c)
    x_copies = []
    for ds in range(1, S):
        c = remote(pack.at[e], xbuf.at[0, mine_rows], x_send.at[0, ds], x_recv.at[0, ds], ds, 0)
        c.start()
        x_copies.append(c)
    own = pltpu.make_async_copy(pack.at[e], xbuf.at[0, mine_rows], own_sem.at[0])
    own.start()

    rows_out, rows_in = E * S * RP, F * rows
    out_row = iota((rows_out, 1), 0)
    inner = lax.rem(out_row, RP)
    which = lax.div(out_row, RP)
    ds_of = lax.rem(which, S)
    de_of = lax.div(which, S)
    f_of = lax.div(inner, cap)
    slot_of = lax.rem(inner, cap)
    s_of = lax.rem(s + S - ds_of, S)
    e_of = lax.rem(e + E - de_of, E)
    from_row = f_of * rows + s_of * RB + e_of * cap + slot_of
    from_row = jnp.where(inner < F * cap, from_row, -1)
    perm = onehot(from_row == iota((rows_out, rows_in), 1))

    m_own = members(mine)
    before = dot(onehot(iota((T, T), 1) < iota((T, T), 0)), m_own)
    picks = []
    wide = iota((T, E * RP), 1)
    at = []
    for k in range(2):
        rk = mine[:, k:k + 1]
        slot = jnp.sum(jnp.where(rk == lanes, before, F32(0.0)), axis=1, keepdims=True)
        rel = rk - e
        rel = jnp.where(rel < 0, rel + E, rel)
        at.append(rel * RP + slot.astype(jnp.int32))
    for f in range(F):
        for k in range(2):
            picks.append(onehot(at[k] + f * cap == wide))
    pick = jnp.concatenate(picks, axis=0)

    square = jnp.zeros((rows, 1), F32)
    sends = []
    for r in range(E):
        if r + 1 < E:
            z_copies[r + 1].wait()
            for ds in range(1, S):
                c = remote(xbuf.at[r + 1, mine_rows], xbuf.at[r + 1, mine_rows],
                           x_send.at[r + 1, ds], x_recv.at[r + 1, ds], ds, 0)
                c.start()
                x_copies.append(c)
        if r == 0:
            own.wait()
        for c in x_copies[r * (S - 1):(r + 1) * (S - 1)]:
            c.wait()
        w_copy(r).wait()
        x = xbuf[r]
        xf = x.astype(F32)
        square = square + jnp.sum(xf * xf, axis=-1, keepdims=True)
        if r < E - 1:
            def body(i, carry, r=r, x=x):
                cols = pl.ds(pl.multiple_of(i * tile, tile), tile)
                part = dot(x, wbuf[r, :, cols])
                if r == 0:
                    acc[:, cols] = part
                else:
                    acc[:, cols] += part
                return carry

            lax.fori_loop(0, ff // tile, body, 0)
        else:
            factor = lax.rsqrt(square / depth + 1e-05)
            for st, (c0, n) in enumerate(steps):
                folded = []
                for f in range(F):
                    cols = slice(f * nc + c0, f * nc + c0 + n)
                    part = dot(x, wbuf[r, :, cols])
                    if r > 0:
                        part = part + acc[:, cols]
                    part = part * factor
                    folded.append((part / (1.0 + jnp.exp(-part))).astype(BF16))
                moved = dot(perm, jnp.concatenate(folded, axis=0)).astype(BF16)
                for de in reversed(range(E)):
                    for ds in reversed(range(S)):
                        base = (de * S + ds) * RP
                        block = moved[base:base + RP]
                        if ds or de:
                            sendbuf[de, ds, :, c0:c0 + n] = block
                        else:
                            recv[0, 0, :, c0:c0 + n] = block
                for de in reversed(range(E)):
                    for ds in reversed(range(S)):
                        if ds or de:
                            c = remote(sendbuf.at[de, ds, :, pl.ds(c0, n)],
                                       recv.at[ds, de, :, pl.ds(c0, n)],
                                       b_send.at[st, de, ds], b_recv.at[st, de, ds], ds, de)
                            c.start()
                            sends.append((st, ds, c))

    g0, g1 = gates_ref[:, 0:1], gates_ref[:, 1:2]
    for st, (c0, n) in enumerate(steps):
        for ds in range(S):
            for a, b, c in sends:
                if a == st and b == ds:
                    c.wait()
            got = recv[ds, :, :, c0:c0 + n].reshape(E * RP, n)
            res = dot(pick, got)
            base = lax.rem(s + ds, S) * ff
            for f in range(F):
                lo = 2 * f * T
                mix = g0 * res[lo:lo + T] + g1 * res[lo + T:lo + 2 * T]
                cols = pl.ds(pl.multiple_of(base + (f * nc + c0), 128), n)
                out_ref[:, cols] = mix.astype(BF16)


def shards(queries, keys, values, lengths, routes, gates, w_up):
    S, E = lax.axis_size("seq"), lax.axis_size("expert")
    q_rows, width = queries.shape
    shard = keys.shape[0]
    w = w_up.reshape(w_up.shape[1], w_up.shape[2])
    depth, ff = w.shape
    T = routes.shape[0]
    cap = max(2, 3 * q_rows // (E * E))
    RB = up(E * cap, 16)
    choices = [f for f in range(1, ff // 128 + 1) if ff % (f * 128) == 0]
    F = min(choices, key=lambda f: up(f * cap, 16) * (ff // f))
    RP = up(F * cap, 16)
    nc = ff // F
    half = up(nc // 2, 256)
    steps = [(0, nc)] if half >= nc else [(0, half), (half, nc - half)]
    tile = 512 if ff % 512 == 0 else 128
    window = shard * S // 2
    pieces = []
    for d in range(1, S):
        first = max(0, (d + 1) * shard - q_rows - window + 1) // 16 * 16
        if first < shard:
            pieces.append((d, first))
    kv_rows = sum(shard - first for _, first in pieces)
    cfg = (S, E, lengths.shape[0], cap, RB, F, RP, nc, steps, pieces, tile)
    vmem = pl.BlockSpec(memory_space=pltpu.VMEM)
    dma = pltpu.SemaphoreType.DMA
    return pl.pallas_call(
        functools.partial(kernel, cfg),
        out_shape=jax.ShapeDtypeStruct((T, S * ff), BF16),
        in_specs=[pl.BlockSpec(memory_space=pltpu.SMEM), vmem, vmem, vmem, vmem, vmem,
                  pl.BlockSpec(memory_space=pl.ANY)],
        out_specs=vmem,
        scratch_shapes=[
            pltpu.VMEM((E, width, ff), BF16),
            pltpu.VMEM((kv_rows, keys.shape[1]), BF16),
            pltpu.VMEM((kv_rows, keys.shape[1]), BF16),
            pltpu.VMEM((E, T, 2), jnp.int32),
            pltpu.VMEM((E, RB, width), BF16),
            pltpu.VMEM((E, S * RB, width), BF16),
            pltpu.VMEM((S * RB, ff), F32),
            pltpu.VMEM((E, S, RP, nc), BF16),
            pltpu.VMEM((S, E, RP, nc), BF16),
            dma((E,)),
            dma((2 * len(pieces),)),
            dma((2 * len(pieces),)),
            dma((E,)), dma((E,)), dma((E,)), dma((E,)),
            dma((E, S)), dma((E, S)),
            dma((1,)),
            dma((len(steps), E, S)), dma((len(steps), E, S)),
        ],
        compiler_params=pltpu.CompilerParams(
            collective_id=0, has_side_effects=True, vmem_limit_bytes=60 * 1024 * 1024
        ),
    )(lengths, queries, keys, values, routes, gates, w)


def solution(mesh):
    placed = (
        P(("dp", "seq"), "expert"),
        P(("dp", "seq"), "expert"),
        P(("dp", "seq"), "expert"),
        P("dp"),
        P(("dp", "seq", "expert"), None),
        P(("dp", "seq", "expert"), None),
        P("expert", None, "seq"),
    )
    return jax.shard_map(
        shards,
        mesh=mesh,
        in_specs=placed,
        out_specs=P(("dp", "seq", "expert"), None),
        check_vma=False,
    )
```

time: 99 us -> 47.9 us (0.48)
  Pallas kernels: 0 us -> 43.3 us
  blocking collectives: 39.5 us -> 0 us
  waiting for transfers between devices: 27 us -> 0 us
  matrix products: 14.2 us -> 0 us
  starting transfers between devices: 8.68 us -> 0 us
  other arithmetic: 2.8 us -> 0 us
  local copies, waits for them, and re-layouts: 6.17 us -> 4.34 us
    pallas_call x0 -> x1, Pallas kernels: none -> 43.3 us  [shards(): pl.pallas_call(functools.partial(kernel, cfg), out_shape=jax.ShapeDtypeSt...]
    all_to_all x2 -> x0, waiting for transfers between devices: 27 us -> none  [the longest x1 21.6 us: shards(): lax.all_to_all(act, ('seq', 'expert'), split_axis=0, concat_axis=0, tiled...]
    all_to_all x1 -> x0, blocking collectives: 26.8 us -> none  [shards(): lax.all_to_all(copies, ('seq', 'expert'), split_axis=0, concat_axis=0, ti...]
    dot_general x5 -> x0, matrix products: 14.2 us -> none  [the longest x1 12.2 us: shards(): upper = jnp.dot(incoming, w_up[0], preferred_element_type=jnp.float32)]
    all_gather x2 -> x0, blocking collectives: 12.8 us -> none  [the longest x1 7.12 us: shards(): k_piece = lax.all_gather(keys, 'seq', axis=0, tiled=True)]
    all_to_all x2 -> x0, starting transfers between devices: 8.68 us -> none  [the longest x1 5.13 us: shards(): lax.all_to_all(attended, 'expert', split_axis=0, concat_axis=1, tiled=True)]
    unnamed x9 -> x3, local copies, waits for them, and re-layouts: 1.2 us -> 4.34 us
    reshape x5 -> x0, local copies, waits for them, and re-layouts: 2.41 us -> none  [the longest x1 0.98 us: shards(): q_split = queries.reshape(q_rows, kv_local, group, HD)]
  transfers between devices with their start and end apart: 2 -> 0, of which waited for: 2 -> 0; matrix products, arithmetic and copies ran while one was open for 1% -> 0% of each run, Pallas kernels for 0% -> 0%
where the time goes in v1:
time: 47.9 us; the launch traced here: 47.7 us
  Pallas kernels  43.3 us (90%)
  local copies, waits for them, and re-layouts  4.34 us (9%)
    pallas_call x1, Pallas kernels, shards(): pl.pallas_call(functools.partial(kernel, cfg), out_shape=jax.ShapeDtypeSt...  43.3 us
    unnamed x3, local copies, waits for them, and re-layouts  4.34 us

profile of v1, /device:TPU:0, one launch (start us, length us, event | category | flops | bytes accessed | tf_op | source)
XLA Modules:
  0.0 47.7 jit_solution(3943517008842859365)
XLA Ops:
  0.0 1.4 %copy.8.routes_ref = s32[16,2]{1,0:T(8,128)} copy(s32[16,2]{0,1:T(2,128)} %param.11) | data formatting | bytes 256 | tf_op args[4]
  1.4 1.4 %copy.9.gates_ref = f32[16,2]{1,0:T(8,128)} copy(f32[16,2]{0,1:T(2,128)} %param.12) | data formatting | bytes 256 | tf_op args[5]
  2.7 43.3 %shard_map.73 = bf16[16,7168]{1,0:T(8,128)(2,1)} custom-call(s32[8]{0:T(128)} %len_ref.1, bf16[64,1024]{1,0:T(8,128)(2,1)} %q_ref.1, bf16[256,256]{1,0:T(8,128)(2,1)} %k_ref.1, bf16[256,256]{1,0:T(8,128)(2,1)} %v_ref.1, s32[16,2]{1,0:T(8,128)} %copy.8.routes_ref, f32[16,2]{1,0:T(8,128)} %copy.9.gates_ref, bf16[4096,3584]{1,0:T(8,128)(2,1)} %bitcast.1), custom_call_target="tpu_custom_call" | custom-call | tf_op jit(solution)/shard_map/pallas_call | solution.py:327
  46.0 1.6 %copy.11 = bf16[16,7168]{1,0:T(8,128)(2,1)} copy(bf16[16,7168]{1,0:T(8,128)(2,1)} %shard_map.73) | data formatting | bytes 458752

commit v2 on v1

--- a/solution.py
+++ b/solution.py
@@ -44,7 +44,7 @@
     shard = k_ref.shape[0]
     kvl = k_ref.shape[1] // HD
     group = width // HD // kvl
-    T = routes_ref.shape[0]
+    T = routes_ref.shape[1]
     ff = w_hbm.shape[1]
     depth = w_hbm.shape[0]
     scale = 1.0 / HD**0.5
@@ -123,22 +123,22 @@
 
     for c in r_copies:
         c.wait()
-    lanes = iota((1, 128), 1)
     mine = routes_ref[...]
+    names = iota((up(E, 8), 1), 0)
 
     def members(rt):
-        return onehot((rt[:, 0:1] == lanes) | (rt[:, 1:2] == lanes))
-
-    eye = onehot(iota((up(E, 8), 128), 0) == iota((up(E, 8), 128), 1))
+        return onehot((rt[0:1, :] == names) | (rt[1:2, :] == names))
+
     upper = onehot(iota((T, T), 0) < iota((T, T), 1))
     blocks = []
     for de in range(E):
-        m = members(mine if de == 0 else rbuf[de])
-        mt = lax.dot_general(eye, m, NT, preferred_element_type=F32)
-        cnt = dot(mt.astype(BF16), upper)
+        mt = members(mine if de == 0 else rbuf[de])
+        cnt = dot(mt, upper)
         blk = lax.rem(e + de, E)
         place = jnp.where(mt > 0.5, cnt + (blk * cap).astype(F32), F32(-1.0))
         blocks.append((place, blk))
+        if de == 0:
+            before = cnt
     Q = q_rows
     total_place = jnp.zeros((up(E, 8), Q), F32)
     for place, blk in blocks:
@@ -208,17 +208,20 @@
     from_row = jnp.where(inner < F * cap, from_row, -1)
     perm = onehot(from_row == iota((rows_out, rows_in), 1))
 
-    m_own = members(mine)
-    before = dot(onehot(iota((T, T), 1) < iota((T, T), 0)), m_own)
+    diagonal = iota((T, T), 0) == iota((T, T), 1)
+
+    def column(row):
+        return jnp.sum(jnp.where(diagonal, row, jnp.zeros_like(row)), axis=1, keepdims=True)
+
     picks = []
     wide = iota((T, E * RP), 1)
     at = []
     for k in range(2):
-        rk = mine[:, k:k + 1]
-        slot = jnp.sum(jnp.where(rk == lanes, before, F32(0.0)), axis=1, keepdims=True)
+        rk = mine[k:k + 1, :]
+        slot = jnp.sum(jnp.where(rk == names, before, F32(0.0)), axis=0, keepdims=True)
         rel = rk - e
         rel = jnp.where(rel < 0, rel + E, rel)
-        at.append(rel * RP + slot.astype(jnp.int32))
+        at.append(column((rel * RP).astype(F32) + slot).astype(jnp.int32))
     for f in range(F):
         for k in range(2):
             picks.append(onehot(at[k] + f * cap == wide))
@@ -282,7 +285,7 @@
                             c.start()
                             sends.append((st, ds, c))
 
-    g0, g1 = gates_ref[:, 0:1], gates_ref[:, 1:2]
+    g0, g1 = column(gates_ref[0:1, :]), column(gates_ref[1:2, :])
     for st, (c0, n) in enumerate(steps):
         for ds in range(S):
             for a, b, c in sends:
@@ -334,7 +337,7 @@
             pltpu.VMEM((E, width, ff), BF16),
             pltpu.VMEM((kv_rows, keys.shape[1]), BF16),
             pltpu.VMEM((kv_rows, keys.shape[1]), BF16),
-            pltpu.VMEM((E, T, 2), jnp.int32),
+            pltpu.VMEM((E, 2, T), jnp.int32),
             pltpu.VMEM((E, RB, width), BF16),
             pltpu.VMEM((E, S * RB, width), BF16),
             pltpu.VMEM((S * RB, ff), F32),
@@ -351,7 +354,7 @@
         compiler_params=pltpu.CompilerParams(
             collective_id=0, has_side_effects=True, vmem_limit_bytes=60 * 1024 * 1024
         ),
-    )(lengths, queries, keys, values, routes, gates, w)
+    )(lengths, queries, keys, values, routes.T, gates.T, w)
 
 
 def solution(mesh):

time: 47.9 us -> 44 us (0.919)
  local copies, waits for them, and re-layouts: 4.34 us -> 1.64 us
  Pallas kernels: 43.3 us -> 42.2 us
    unnamed x3 -> x1, local copies, waits for them, and re-layouts: 4.34 us -> 1.64 us
    pallas_call x1, Pallas kernels: 43.3 us -> 42.2 us  [shards(): pl.pallas_call(functools.partial(kernel, cfg), out_shape=jax.ShapeDtypeSt...]
where the time goes in v2:
time: 44 us; the launch traced here: 43.9 us
  Pallas kernels  42.2 us (96%)
  local copies, waits for them, and re-layouts  1.64 us (4%)
    pallas_call x1, Pallas kernels, shards(): pl.pallas_call(functools.partial(kernel, cfg), out_shape=jax.ShapeDtypeSt...  42.2 us
    unnamed x1, local copies, waits for them, and re-layouts  1.64 us

profile of v2, /device:TPU:0, one launch (start us, length us, event | category | flops | bytes accessed | tf_op | source)
XLA Modules:
  0.0 43.9 jit_solution(3847329327501773598)
XLA Ops:
  0.0 42.2 %shard_map.73 = bf16[16,7168]{1,0:T(8,128)(2,1)} custom-call(s32[8]{0:T(128)} %len_ref.1, bf16[64,1024]{1,0:T(8,128)(2,1)} %q_ref.1, bf16[256,256]{1,0:T(8,128)(2,1)} %k_ref.1, bf16[256,256]{1,0:T(8,128)(2,1)} %v_ref.1, s32[2,16]{1,0:T(2,128)} %bitcast.4, f32[2,16]{1,0:T(2,128)} %bitcast.5, bf16[4096,3584]{1,0:T(8,128)(2,1)} %bitcast.3), custom_call_target="tpu_custom_call" | custom-call | tf_op jit(solution)/shard_map/pallas_call | solution.py:330
  42.2 1.6 %copy.9 = bf16[16,7168]{1,0:T(8,128)(2,1)} copy(bf16[16,7168]{1,0:T(8,128)(2,1)} %shard_map.73) | data formatting | bytes 458752

commit v3 on v2

--- a/solution.py
+++ b/solution.py
@@ -32,10 +32,11 @@
 
 def kernel(
     cfg,
-    len_ref, q_ref, k_ref, v_ref, routes_ref, gates_ref, w_hbm, out_ref,
+    len_hbm, q_hbm, k_hbm, v_hbm, routes_hbm, gates_hbm, w_hbm, out_hbm,
+    len_ref, q_ref, k_ref, v_ref, routes_ref, gates_ref, out_ref,
     wbuf, kbuf, vbuf, rbuf, pack, xbuf, acc, sendbuf, recv,
-    w_sem, kv_send, kv_recv, r_send, r_recv, z_send, z_recv, x_send, x_recv,
-    own_sem, b_send, b_recv,
+    in_sem, w_sem, kv_send, kv_recv, r_send, r_recv, z_send, z_recv, x_send, x_recv,
+    own_sem, b_send, b_recv, out_sem,
 ):
     S, E, ndoc, cap, RB, F, RP, nc, steps, pieces, tile = cfg
     s = lax.axis_index("seq")
@@ -48,7 +49,6 @@
     ff = w_hbm.shape[1]
     depth = w_hbm.shape[0]
     scale = 1.0 / HD**0.5
-    rows = S * RB
 
     def at_s(d):
         return lax.rem(s + S - d, S)
@@ -71,8 +71,18 @@
             w_hbm.at[pl.ds(pl.multiple_of(src * width, width), width)], wbuf.at[r], w_sem.at[r]
         )
 
+    ins = []
+    for i, (src, dst) in enumerate((
+        (k_hbm, k_ref), (v_hbm, v_ref), (routes_hbm, routes_ref), (q_hbm, q_ref),
+        (len_hbm, len_ref), (gates_hbm, gates_ref),
+    )):
+        c = pltpu.make_async_copy(src, dst, in_sem.at[i])
+        c.start()
+        ins.append(c)
     for r in range(E):
         w_copy(r).start()
+    for c in ins[:3]:
+        c.wait()
     pl.semaphore_wait(barrier, S * E - 1)
 
     def remote(src, dst, ssem, rsem, ds, de):
@@ -99,6 +109,8 @@
         c.start()
         r_copies.append(c)
 
+    for c in ins[3:]:
+        c.wait()
     qn = group * q_rows
     qpos = s * shard + shard - q_rows + lax.rem(iota((qn, 1), 0), q_rows)
     docstart = jnp.zeros((qn, 1), jnp.int32)
@@ -152,6 +164,28 @@
 
     for c in kv_copies:
         c.wait()
+    hw = group * HD
+    z_copies, x_copies, own_copies = {}, {}, []
+
+    def relay(r, h, src):
+        for ds in range(1, S):
+            c = remote(src, xbuf.at[S - ds, r, :, pl.ds(h * hw, hw)],
+                       x_send.at[h, r, ds], x_recv.at[h, r, S - ds], ds, 0)
+            c.start()
+            x_copies[h, r, ds] = c
+
+    def send_head(h):
+        part = pl.ds(h * hw, hw)
+        for r in range(1, E):
+            c = remote(pack.at[at_e(r), :, part], xbuf.at[0, r, :, part],
+                       z_send.at[h, r], z_recv.at[h, r], 0, r)
+            c.start()
+            z_copies[h, r] = c
+        relay(0, h, pack.at[e, :, part])
+        own = pltpu.make_async_copy(pack.at[e, :, part], xbuf.at[0, 0, :, part], own_sem.at[h])
+        own.start()
+        own_copies.append(own)
+
     for h in range(kvl):
         q = queries[h]
         hs = slice(h * HD, (h + 1) * HD)
@@ -178,33 +212,13 @@
             packed = dot(selector, att[g * q_rows:(g + 1) * q_rows]).astype(BF16)
             for x in range(E):
                 pack[x, :, cols] = packed[x * RB:(x + 1) * RB]
-
-    mine_rows = pl.ds(pl.multiple_of(s * RB, RB), RB)
-
-    z_copies = [None]
-    for r in range(1, E):
-        c = remote(pack.at[at_e(r)], xbuf.at[r, mine_rows], z_send.at[r], z_recv.at[r], 0, r)
-        c.start()
-        z_copies.append(c)
-    x_copies = []
-    for ds in range(1, S):
-        c = remote(pack.at[e], xbuf.at[0, mine_rows], x_send.at[0, ds], x_recv.at[0, ds], ds, 0)
-        c.start()
-        x_copies.append(c)
-    own = pltpu.make_async_copy(pack.at[e], xbuf.at[0, mine_rows], own_sem.at[0])
-    own.start()
-
-    rows_out, rows_in = E * S * RP, F * rows
+        send_head(h)
+
+    rows_out, rows_in = E * RP, F * RB
     out_row = iota((rows_out, 1), 0)
     inner = lax.rem(out_row, RP)
-    which = lax.div(out_row, RP)
-    ds_of = lax.rem(which, S)
-    de_of = lax.div(which, S)
-    f_of = lax.div(inner, cap)
-    slot_of = lax.rem(inner, cap)
-    s_of = lax.rem(s + S - ds_of, S)
-    e_of = lax.rem(e + E - de_of, E)
-    from_row = f_of * rows + s_of * RB + e_of * cap + slot_of
+    e_of = lax.rem(e + E - lax.div(out_row, RP), E)
+    from_row = lax.div(inner, cap) * RB + e_of * cap + lax.rem(inner, cap)
     from_row = jnp.where(inner < F * cap, from_row, -1)
     perm = onehot(from_row == iota((rows_out, rows_in), 1))
 
@@ -227,24 +241,45 @@
             picks.append(onehot(at[k] + f * cap == wide))
     pick = jnp.concatenate(picks, axis=0)
 
-    square = jnp.zeros((rows, 1), F32)
-    sends = []
+    sends = {}
+
+    def squares(g, r):
+        xf = xbuf[g, r].astype(F32)
+        return jnp.sum(xf * xf, axis=-1, keepdims=True)
+
+    def give_back(g, square, product):
+        factor = lax.rsqrt(square / depth + 1e-05)
+        for st, (c0, n) in enumerate(steps):
+            folded = []
+            for f in range(F):
+                part = product(slice(f * nc + c0, f * nc + c0 + n)) * factor
+                folded.append((part / (1.0 + jnp.exp(-part))).astype(BF16))
+            moved = dot(perm, jnp.concatenate(folded, axis=0)).astype(BF16)
+            for de in range(E):
+                block = moved[de * RP:(de + 1) * RP]
+                if g or de:
+                    sendbuf[de, g, :, c0:c0 + n] = block
+                else:
+                    recv[0, 0, :, c0:c0 + n] = block
+            for de in reversed(range(E)):
+                if g or de:
+                    c = remote(sendbuf.at[de, g, :, pl.ds(c0, n)],
+                               recv.at[g, de, :, pl.ds(c0, n)],
+                               b_send.at[st, de, g], b_recv.at[st, de, g], g, de)
+                    c.start()
+                    sends[st, de, g] = c
+
+    square = jnp.zeros((RB, 1), F32)
     for r in range(E):
-        if r + 1 < E:
-            z_copies[r + 1].wait()
-            for ds in range(1, S):
-                c = remote(xbuf.at[r + 1, mine_rows], xbuf.at[r + 1, mine_rows],
-                           x_send.at[r + 1, ds], x_recv.at[r + 1, ds], ds, 0)
-                c.start()
-                x_copies.append(c)
-        if r == 0:
-            own.wait()
-        for c in x_copies[r * (S - 1):(r + 1) * (S - 1)]:
-            c.wait()
+        for h in range(kvl):
+            if r:
+                z_copies[h, r].wait()
+                relay(r, h, xbuf.at[0, r, :, pl.ds(h * hw, hw)])
+            else:
+                own_copies[h].wait()
         w_copy(r).wait()
-        x = xbuf[r]
-        xf = x.astype(F32)
-        square = square + jnp.sum(xf * xf, axis=-1, keepdims=True)
+        square = square + squares(0, r)
+        x = xbuf[0, r]
         if r < E - 1:
             def body(i, carry, r=r, x=x):
                 cols = pl.ds(pl.multiple_of(i * tile, tile), tile)
@@ -257,48 +292,48 @@
 
             lax.fori_loop(0, ff // tile, body, 0)
         else:
-            factor = lax.rsqrt(square / depth + 1e-05)
-            for st, (c0, n) in enumerate(steps):
-                folded = []
-                for f in range(F):
-                    cols = slice(f * nc + c0, f * nc + c0 + n)
-                    part = dot(x, wbuf[r, :, cols])
-                    if r > 0:
-                        part = part + acc[:, cols]
-                    part = part * factor
-                    folded.append((part / (1.0 + jnp.exp(-part))).astype(BF16))
-                moved = dot(perm, jnp.concatenate(folded, axis=0)).astype(BF16)
-                for de in reversed(range(E)):
-                    for ds in reversed(range(S)):
-                        base = (de * S + ds) * RP
-                        block = moved[base:base + RP]
-                        if ds or de:
-                            sendbuf[de, ds, :, c0:c0 + n] = block
-                        else:
-                            recv[0, 0, :, c0:c0 + n] = block
-                for de in reversed(range(E)):
-                    for ds in reversed(range(S)):
-                        if ds or de:
-                            c = remote(sendbuf.at[de, ds, :, pl.ds(c0, n)],
-                                       recv.at[ds, de, :, pl.ds(c0, n)],
-                                       b_send.at[st, de, ds], b_recv.at[st, de, ds], ds, de)
-                            c.start()
-                            sends.append((st, ds, c))
+            def last(cols, r=r, x=x):
+                part = dot(x, wbuf[r, :, cols])
+                return part + acc[:, cols] if r else part
+
+            give_back(0, square, last)
+    for g in range(1, S):
+        square = jnp.zeros((RB, 1), F32)
+        for r in range(E):
+            for h in range(kvl):
+                x_copies[h, r, S - g].wait_recv()
+            square = square + squares(g, r)
+
+        def whole(cols, g=g):
+            part = dot(xbuf[g, 0], wbuf[0, :, cols])
+            for r in range(1, E):
+                part = part + dot(xbuf[g, r], wbuf[r, :, cols])
+            return part
+
+        give_back(g, square, whole)
+    for c in x_copies.values():
+        c.wait_send()
 
     g0, g1 = column(gates_ref[0:1, :]), column(gates_ref[1:2, :])
-    for st, (c0, n) in enumerate(steps):
-        for ds in range(S):
-            for a, b, c in sends:
-                if a == st and b == ds:
-                    c.wait()
-            got = recv[ds, :, :, c0:c0 + n].reshape(E * RP, n)
+    outs = []
+    for g in range(S):
+        base = pl.multiple_of(lax.rem(s + g, S) * ff, 128)
+        for st, (c0, n) in enumerate(steps):
+            for de in range(E):
+                if g or de:
+                    sends[st, de, g].wait()
+            got = recv[g, :, :, c0:c0 + n].reshape(E * RP, n)
             res = dot(pick, got)
-            base = lax.rem(s + ds, S) * ff
             for f in range(F):
                 lo = 2 * f * T
                 mix = g0 * res[lo:lo + T] + g1 * res[lo + T:lo + 2 * T]
-                cols = pl.ds(pl.multiple_of(base + (f * nc + c0), 128), n)
-                out_ref[:, cols] = mix.astype(BF16)
+                cols = slice(f * nc + c0, f * nc + c0 + n)
+                out_ref[g, :, cols] = mix.astype(BF16)
+        c = pltpu.make_async_copy(out_ref.at[g], out_hbm.at[:, pl.ds(base, ff)], out_sem.at[g])
+        c.start()
+        outs.append(c)
+    for c in outs:
+        c.wait()
 
 
 def shards(queries, keys, values, lengths, routes, gates, w_up):
@@ -314,8 +349,8 @@
     F = min(choices, key=lambda f: up(f * cap, 16) * (ff // f))
     RP = up(F * cap, 16)
     nc = ff // F
-    half = up(nc // 2, 256)
-    steps = [(0, nc)] if half >= nc else [(0, half), (half, nc - half)]
+    cuts = list(range(0, max(nc - 255, 1), 256))
+    steps = [(c, (cuts + [nc])[i + 1] - c) for i, c in enumerate(cuts)]
     tile = 512 if ff % 512 == 0 else 128
     window = shard * S // 2
     pieces = []
@@ -325,31 +360,39 @@
             pieces.append((d, first))
     kv_rows = sum(shard - first for _, first in pieces)
     cfg = (S, E, lengths.shape[0], cap, RB, F, RP, nc, steps, pieces, tile)
-    vmem = pl.BlockSpec(memory_space=pltpu.VMEM)
+    kvl = keys.shape[1] // HD
     dma = pltpu.SemaphoreType.DMA
     return pl.pallas_call(
         functools.partial(kernel, cfg),
         out_shape=jax.ShapeDtypeStruct((T, S * ff), BF16),
-        in_specs=[pl.BlockSpec(memory_space=pltpu.SMEM), vmem, vmem, vmem, vmem, vmem,
-                  pl.BlockSpec(memory_space=pl.ANY)],
-        out_specs=vmem,
+        in_specs=[pl.BlockSpec(memory_space=pl.ANY)] * 7,
+        out_specs=pl.BlockSpec(memory_space=pl.ANY),
         scratch_shapes=[
+            pltpu.SMEM(lengths.shape, jnp.int32),
+            pltpu.VMEM(queries.shape, BF16),
+            pltpu.VMEM(keys.shape, BF16),
+            pltpu.VMEM(values.shape, BF16),
+            pltpu.VMEM((2, T), jnp.int32),
+            pltpu.VMEM((2, T), F32),
+            pltpu.VMEM((S, T, ff), BF16),
             pltpu.VMEM((E, width, ff), BF16),
             pltpu.VMEM((kv_rows, keys.shape[1]), BF16),
             pltpu.VMEM((kv_rows, keys.shape[1]), BF16),
             pltpu.VMEM((E, 2, T), jnp.int32),
             pltpu.VMEM((E, RB, width), BF16),
-            pltpu.VMEM((E, S * RB, width), BF16),
-            pltpu.VMEM((S * RB, ff), F32),
+            pltpu.VMEM((S, E, RB, width), BF16),
+            pltpu.VMEM((RB, ff), F32),
             pltpu.VMEM((E, S, RP, nc), BF16),
             pltpu.VMEM((S, E, RP, nc), BF16),
+            dma((6,)),
             dma((E,)),
             dma((2 * len(pieces),)),
             dma((2 * len(pieces),)),
-            dma((E,)), dma((E,)), dma((E,)), dma((E,)),
-            dma((E, S)), dma((E, S)),
-            dma((1,)),
+            dma((E,)), dma((E,)), dma((kvl, E)), dma((kvl, E)),
+            dma((kvl, E, S)), dma((kvl, E, S)),
+            dma((kvl,)),
             dma((len(steps), E, S)), dma((len(steps), E, S)),
+            dma((S,)),
         ],
         compiler_params=pltpu.CompilerParams(
             collective_id=0, has_side_effects=True, vmem_limit_bytes=60 * 1024 * 1024

time: 44 us -> 43.2 us (0.982)
  Pallas kernels: 42.2 us -> 41.4 us
    pallas_call x1, Pallas kernels: 42.2 us -> 41.4 us  [shards(): pl.pallas_call(functools.partial(kernel, cfg), out_shape=jax.ShapeDtypeSt...]
where the time goes in v3:
time: 43.2 us; the launch traced here: 43.1 us
  Pallas kernels  41.4 us (96%)
  local copies, waits for them, and re-layouts  1.64 us (4%)
    pallas_call x1, Pallas kernels, shards(): pl.pallas_call(functools.partial(kernel, cfg), out_shape=jax.ShapeDtypeSt...  41.4 us
    unnamed x1, local copies, waits for them, and re-layouts  1.64 us

profile of v3, /device:TPU:0, one launch (start us, length us, event | category | flops | bytes accessed | tf_op | source)
XLA Modules:
  0.0 43.1 jit_solution(1613368988487165530)
XLA Ops:
  0.0 41.4 %shard_map.73 = bf16[16,7168]{1,0:T(8,128)(2,1)} custom-call(s32[8]{0:T(128)} %len_hbm.1, bf16[64,1024]{1,0:T(8,128)(2,1)} %q_hbm.1, bf16[256,256]{1,0:T(8,128)(2,1)} %k_hbm.1, bf16[256,256]{1,0:T(8,128)(2,1)} %v_hbm.1, s32[2,16]{1,0:T(2,128)} %bitcast.4, f32[2,16]{1,0:T(2,128)} %bitcast.5, bf16[4096,3584]{1,0:T(8,128)(2,1)} %bitcast.3), custom_call_target="tpu_custom_call" | custom-call | tf_op jit(solution)/shard_map/pallas_call | solution.py:365
  41.5 1.6 %copy.9 = bf16[16,7168]{1,0:T(8,128)(2,1)} copy(bf16[16,7168]{1,0:T(8,128)(2,1)} %shard_map.73) | data formatting | bytes 458752

commit v4 on v3

--- a/solution.py
+++ b/solution.py
@@ -131,7 +131,11 @@
             [q_ref[:, (h * group + g) * HD:(h * group + g + 1) * HD] for g in range(group)], axis=0
         )
         queries.append(q)
-        local.append(masked(q, k_ref[:, h * HD:(h + 1) * HD], s * shard))
+        sc = masked(q, k_ref[:, h * HD:(h + 1) * HD], s * shard)
+        peak = jnp.max(sc, axis=-1, keepdims=True)
+        wt = jnp.exp(sc - peak)
+        local.append((peak, jnp.sum(wt, axis=-1, keepdims=True),
+                      dot(wt.astype(BF16), v_ref[:, h * HD:(h + 1) * HD])))
 
     for c in r_copies:
         c.wait()
@@ -189,23 +193,18 @@
     for h in range(kvl):
         q = queries[h]
         hs = slice(h * HD, (h + 1) * HD)
-        parts = [(local[h], v_ref[:, hs])]
+        peak, total, got = local[h]
         offset = 0
         for d, first in pieces:
             n = shard - first
-            parts.append((masked(q, kbuf[offset:offset + n, hs], (s - d) * shard + first),
-                          vbuf[offset:offset + n, hs]))
+            sc = masked(q, kbuf[offset:offset + n, hs], (s - d) * shard + first)
+            higher = jnp.maximum(peak, jnp.max(sc, axis=-1, keepdims=True))
+            wt = jnp.exp(sc - higher)
+            fade = jnp.exp(peak - higher)
+            total = total * fade + jnp.sum(wt, axis=-1, keepdims=True)
+            got = got * fade + dot(wt.astype(BF16), vbuf[offset:offset + n, hs])
+            peak = higher
             offset += n
-        peak = jnp.max(parts[0][0], axis=-1, keepdims=True)
-        for sc, _ in parts[1:]:
-            peak = jnp.maximum(peak, jnp.max(sc, axis=-1, keepdims=True))
-        total, got = None, None
-        for sc, v in parts:
-            wt = jnp.exp(sc - peak)
-            t = jnp.sum(wt, axis=-1, keepdims=True)
-            o = dot(wt.astype(BF16), v)
-            total = t if total is None else total + t
-            got = o if got is None else got + o
         att = (got / total).astype(BF16)
         for g in range(group):
             cols = slice((h * group + g) * HD, (h * group + g + 1) * HD)

time: 43.2 us -> 43.7 us (1.012)
  Pallas kernels: 41.4 us -> 41.9 us
    pallas_call x1, Pallas kernels: 41.4 us -> 41.9 us  [shards(): pl.pallas_call(functools.partial(kernel, cfg), out_shape=jax.ShapeDtypeSt...]
where the time goes in v4:
time: 43.7 us; the launch traced here: 43.6 us
  Pallas kernels  41.9 us (96%)
  local copies, waits for them, and re-layouts  1.64 us (4%)
    pallas_call x1, Pallas kernels, shards(): pl.pallas_call(functools.partial(kernel, cfg), out_shape=jax.ShapeDtypeSt...  41.9 us
    unnamed x1, local copies, waits for them, and re-layouts  1.64 us

profile of v4, /device:TPU:0, one launch (start us, length us, event | category | flops | bytes accessed | tf_op | source)
XLA Modules:
  0.0 43.6 jit_solution(2719364022655754473)
XLA Ops:
  0.0 41.9 %shard_map.73 = bf16[16,7168]{1,0:T(8,128)(2,1)} custom-call(s32[8]{0:T(128)} %len_hbm.1, bf16[64,1024]{1,0:T(8,128)(2,1)} %q_hbm.1, bf16[256,256]{1,0:T(8,128)(2,1)} %k_hbm.1, bf16[256,256]{1,0:T(8,128)(2,1)} %v_hbm.1, s32[2,16]{1,0:T(2,128)} %bitcast.4, f32[2,16]{1,0:T(2,128)} %bitcast.5, bf16[4096,3584]{1,0:T(8,128)(2,1)} %bitcast.3), custom_call_target="tpu_custom_call" | custom-call | tf_op jit(solution)/shard_map/pallas_call | solution.py:364
  41.9 1.6 %copy.9 = bf16[16,7168]{1,0:T(8,128)(2,1)} copy(bf16[16,7168]{1,0:T(8,128)(2,1)} %shard_map.73) | data formatting | bytes 458752

commit v5 on v4

--- a/solution.py
+++ b/solution.py
@@ -79,8 +79,6 @@
         c = pltpu.make_async_copy(src, dst, in_sem.at[i])
         c.start()
         ins.append(c)
-    for r in range(E):
-        w_copy(r).start()
     for c in ins[:3]:
         c.wait()
     pl.semaphore_wait(barrier, S * E - 1)
@@ -111,6 +109,8 @@
 
     for c in ins[3:]:
         c.wait()
+    for r in range(E):
+        w_copy(r).start()
     qn = group * q_rows
     qpos = s * shard + shard - q_rows + lax.rem(iota((qn, 1), 0), q_rows)
     docstart = jnp.zeros((qn, 1), jnp.int32)

time: 43.7 us -> 39.8 us (0.911)
  Pallas kernels: 41.9 us -> 38 us
    pallas_call x1, Pallas kernels: 41.9 us -> 38 us  [shards(): pl.pallas_call(functools.partial(kernel, cfg), out_shape=jax.ShapeDtypeSt...]
where the time goes in v5:
time: 39.8 us; the launch traced here: 39.7 us
  Pallas kernels  38 us (95%)
  local copies, waits for them, and re-layouts  1.64 us (4%)
    pallas_call x1, Pallas kernels, shards(): pl.pallas_call(functools.partial(kernel, cfg), out_shape=jax.ShapeDtypeSt...  38 us
    unnamed x1, local copies, waits for them, and re-layouts  1.64 us

profile of v5, /device:TPU:0, one launch (start us, length us, event | category | flops | bytes accessed | tf_op | source)
XLA Modules:
  0.0 39.7 jit_solution(6061905114520151197)
XLA Ops:
  0.0 38.0 %shard_map.73 = bf16[16,7168]{1,0:T(8,128)(2,1)} custom-call(s32[8]{0:T(128)} %len_hbm.1, bf16[64,1024]{1,0:T(8,128)(2,1)} %q_hbm.1, bf16[256,256]{1,0:T(8,128)(2,1)} %k_hbm.1, bf16[256,256]{1,0:T(8,128)(2,1)} %v_hbm.1, s32[2,16]{1,0:T(2,128)} %bitcast.4, f32[2,16]{1,0:T(2,128)} %bitcast.5, bf16[4096,3584]{1,0:T(8,128)(2,1)} %bitcast.3), custom_call_target="tpu_custom_call" | custom-call | tf_op jit(solution)/shard_map/pallas_call | solution.py:364
  38.0 1.6 %copy.9 = bf16[16,7168]{1,0:T(8,128)(2,1)} copy(bf16[16,7168]{1,0:T(8,128)(2,1)} %shard_map.73) | data formatting | bytes 458752
